TPU v7x, 32 devices: a whole 2x2x4 slice. The times are simulated.
32 devices in a mesh: seq: 4 (over y, x), fsdp: 8 (over z, core).
Axes of the slice: x: 2, y: 2, z: 4, core: 2. Of those that a mesh axis runs over, the one named last changes fastest.
Arguments:
- hidden_in: bfloat16 [8, 1024, 2048], P('fsdp', 'seq'), may hold values from -6 to 6
- cotangent: bfloat16 [8, 1024, 2048], P('fsdp', 'seq'), may hold values from -6 to 6
- block_table: int32 [4, 2], replicated, may hold values from 0 to 7, as said below
- first_gain: bfloat16 [2048], P('fsdp'), may hold values from 0.5 to 1.5
- first_bias: bfloat16 [2048], P('fsdp'), may hold values from -3 to 3
- qkv_weight: bfloat16 [2048, 6144], P('fsdp'), may hold values from -0.125 to 0.125
- qkv_bias: bfloat16 [6144], P('fsdp')
- out_weight: bfloat16 [2048, 2048], P('fsdp'), may hold values from -2 to 2
- second_gain: bfloat16 [2048], P('fsdp'), may hold values from 0.5 to 1.5
- second_bias: bfloat16 [2048], P('fsdp'), may hold values from -3 to 3
- gate_weight: bfloat16 [2048, 5632], P('fsdp'), may hold values from -0.125 to 0.125
- up_weight: bfloat16 [2048, 5632], P('fsdp'), may hold values from -0.125 to 0.125
- down_weight: bfloat16 [5632, 2048], P('fsdp'), may hold values from -0.078125 to 0.078125
Outputs:
- block_out: bfloat16 [8, 1024, 2048], P('fsdp', 'seq')
- input_grad: bfloat16 [8, 1024, 2048], P('fsdp', 'seq')
- first_gain_grad: float32 [2048], P('fsdp')
- first_bias_grad: float32 [2048], P('fsdp')
- qkv_weight_grad: float32 [2048, 6144], P('fsdp')
- qkv_bias_grad: float32 [6144], P('fsdp')
- out_weight_grad: float32 [2048, 2048], P('fsdp')
- second_gain_grad: float32 [2048], P('fsdp')
- second_bias_grad: float32 [2048], P('fsdp')
- gate_weight_grad: float32 [2048, 5632], P('fsdp')
- up_weight_grad: float32 [2048, 5632], P('fsdp')
- down_weight_grad: float32 [5632, 2048], P('fsdp')
Inputs may be any that keep to these rules, and one draw needn't show every extreme that they name: `block_table`: row i holds a pair b and 7 - b, in either order; every block number appears once in the table; the same table holds for all sequences.
All inputs are finite; a program needn't handle non-finite values.
Results may differ from a plain program's by a relative error of at most 0.028.
The roundings to bfloat16 on the way count: a program that leaves them out, or rounds other values in their place, can miss the bound.
Values may be sent and summed in bfloat16 or wider, within the bound.
A program may use at most 448 MiB of HBM per device.

v0:
```python
import jax
import jax.numpy as jnp
from jax import lax
from jax.sharding import PartitionSpec as P

HEADS = 32
HD = 64
EPS = 1e-05
ROPE_BASE = 10000.0
NEG = -1e30


def normalize(values):
    centred = values - jnp.mean(values, axis=-1, keepdims=True)
    inverse = lax.rsqrt(jnp.mean(centred * centred, axis=-1, keepdims=True) + EPS)
    return (centred * inverse, inverse)


def norm_back(d_normed, centred_scaled, inverse, gain):
    scaled = d_normed * gain
    return inverse * (
        scaled
        - jnp.mean(scaled, axis=-1, keepdims=True)
        - centred_scaled * jnp.mean(scaled * centred_scaled, axis=-1, keepdims=True)
    )


def rotate(tensor, places, direction):
    head_dim = tensor.shape[-1]
    rotated = head_dim // 4
    half = rotated // 2
    freq = ROPE_BASE ** (-(jnp.arange(half, dtype=jnp.float32) * 2.0) / rotated)
    angle = places.astype(jnp.float32)[:, None] * freq[None, :]
    cosine = jnp.cos(angle)[:, None, :]
    sine = direction * jnp.sin(angle)[:, None, :]
    first = tensor[..., :half]
    second = tensor[..., half:rotated]
    return jnp.concatenate(
        [first * cosine - second * sine, second * cosine + first * sine, tensor[..., rotated:]],
        axis=-1,
    )


def body(
    hidden_in,
    cotangent,
    block_table,
    first_gain,
    first_bias,
    qkv_weight,
    qkv_bias,
    out_weight,
    second_gain,
    second_bias,
    gate_weight,
    up_weight,
    down_weight,
):
    inputs = hidden_in[0].astype(jnp.float32)
    tokens = inputs.shape[0]
    width = inputs.shape[1]
    half_rows = tokens // 2
    heads = HEADS
    head_dim = HD
    group = min(8, heads)
    groups = heads // group
    scale = float(head_dim) ** (-0.5)
    ffn_width = gate_weight.shape[1]
    own_pair = lax.dynamic_slice_in_dim(block_table, lax.axis_index("seq"), 1, 0)[0]
    offsets = jnp.arange(half_rows, dtype=jnp.int32)
    places = (own_pair[:, None] * half_rows + offsets[None, :]).reshape(tokens)
    key_places = (block_table[:, :, None] * half_rows + offsets[None, None, :]).reshape(-1)
    visible = key_places[None, :] <= places[:, None]
    gain_one, bias_one, w_qkv_full, b_qkv_full, w_out_full = (
        lax.all_gather(first_gain, "fsdp", axis=0, tiled=True),
        lax.all_gather(first_bias, "fsdp", axis=0, tiled=True),
        lax.all_gather(qkv_weight, "fsdp", axis=0, tiled=True),
        lax.all_gather(qkv_bias, "fsdp", axis=0, tiled=True),
        lax.all_gather(out_weight, "fsdp", axis=0, tiled=True),
    )
    centred_one, inverse_one = normalize(inputs)
    normed_one = (centred_one * gain_one.astype(jnp.float32) + bias_one.astype(jnp.float32)).astype(
        jnp.bfloat16
    )
    projected = jnp.dot(
        normed_one, w_qkv_full, preferred_element_type=jnp.float32
    ) + b_qkv_full.astype(jnp.float32)
    query = rotate(projected[:, :width].reshape(tokens, heads, head_dim), places, 1.0).astype(
        jnp.bfloat16
    )
    key_rot = rotate(
        projected[:, width : 2 * width].reshape(tokens, heads, head_dim), places, 1.0
    ).astype(jnp.bfloat16)
    value_own = projected[:, 2 * width :].astype(jnp.bfloat16)
    key_all, value_all = (
        lax.all_gather(key_rot.reshape(tokens, width), "seq", axis=0, tiled=True),
        lax.all_gather(value_own, "seq", axis=0, tiled=True),
    )
    key_heads = key_all.reshape(-1, heads, head_dim)
    value_heads = value_all.reshape(-1, heads, head_dim)

    def group_scores(index):
        query_group = lax.dynamic_slice_in_dim(query, index * group, group, 1)
        key_group = lax.dynamic_slice_in_dim(key_heads, index * group, group, 1)
        value_group = lax.dynamic_slice_in_dim(value_heads, index * group, group, 1)
        scores = (
            jnp.einsum("qgd,kgd->gqk", query_group, key_group, preferred_element_type=jnp.float32)
            * scale
        )
        scores = jnp.where(visible[None], scores, NEG)
        return (query_group, key_group, value_group, scores)

    def forward_group(index):
        query_group, key_group, value_group, scores = group_scores(index)
        peak = jnp.max(scores, axis=-1, keepdims=True)
        log_total = peak + jnp.log(jnp.sum(jnp.exp(scores - peak), axis=-1, keepdims=True))
        weights = jnp.exp(scores - log_total).astype(jnp.bfloat16)
        return (
            jnp.einsum("gqk,kgd->qgd", weights, value_group, preferred_element_type=jnp.float32),
            log_total,
        )

    head_out, log_totals = lax.map(forward_group, jnp.arange(groups))
    mixed = head_out.transpose(1, 0, 2, 3).reshape(tokens, width).astype(jnp.bfloat16)
    residual = inputs + jnp.dot(mixed, w_out_full, preferred_element_type=jnp.float32)
    gain_two, bias_two, w_gate_full, w_up_full, w_down_full = (
        lax.all_gather(second_gain, "fsdp", axis=0, tiled=True),
        lax.all_gather(second_bias, "fsdp", axis=0, tiled=True),
        lax.all_gather(gate_weight, "fsdp", axis=0, tiled=True),
        lax.all_gather(up_weight, "fsdp", axis=0, tiled=True),
        lax.all_gather(down_weight, "fsdp", axis=0, tiled=True),
    )
    centred_two, inverse_two = normalize(residual)
    normed_two = (centred_two * gain_two.astype(jnp.float32) + bias_two.astype(jnp.float32)).astype(
        jnp.bfloat16
    )
    gate = jnp.dot(normed_two, w_gate_full, preferred_element_type=jnp.float32)
    upward = jnp.dot(normed_two, w_up_full, preferred_element_type=jnp.float32)
    sigmoid = jax.nn.sigmoid(gate)
    activated = (gate * sigmoid * upward).astype(jnp.bfloat16)
    block_out = (
        residual + jnp.dot(activated, w_down_full, preferred_element_type=jnp.float32)
    ).astype(jnp.bfloat16)
    gain_one, w_qkv_full, w_out_full = (
        lax.all_gather(first_gain, "fsdp", axis=0, tiled=True),
        lax.all_gather(qkv_weight, "fsdp", axis=0, tiled=True),
        lax.all_gather(out_weight, "fsdp", axis=0, tiled=True),
    )
    gain_two, w_gate_full, w_up_full, w_down_full = (
        lax.all_gather(second_gain, "fsdp", axis=0, tiled=True),
        lax.all_gather(gate_weight, "fsdp", axis=0, tiled=True),
        lax.all_gather(up_weight, "fsdp", axis=0, tiled=True),
        lax.all_gather(down_weight, "fsdp", axis=0, tiled=True),
    )
    d_out = cotangent[0].astype(jnp.float32)
    d_branch = d_out.astype(jnp.bfloat16)
    d_activated = jnp.einsum("rd,fd->rf", d_branch, w_down_full, preferred_element_type=jnp.float32)
    d_gate = (d_activated * upward * sigmoid * (1.0 + gate * (1.0 - sigmoid))).astype(jnp.bfloat16)
    d_upward = (d_activated * gate * sigmoid).astype(jnp.bfloat16)
    d_normed_two = jnp.einsum(
        "rf,df->rd", d_gate, w_gate_full, preferred_element_type=jnp.float32
    ) + jnp.einsum("rf,df->rd", d_upward, w_up_full, preferred_element_type=jnp.float32)
    gain_two_grad = jnp.sum(d_normed_two * centred_two, axis=0)
    bias_two_grad = jnp.sum(d_normed_two, axis=0)
    d_residual = d_out + norm_back(
        d_normed_two, centred_two, inverse_two, gain_two.astype(jnp.float32)
    )
    gate_up_rows = jnp.concatenate([d_gate, d_upward], axis=1)
    d_attended = d_residual.astype(jnp.bfloat16)
    normed_slice = normed_two
    gate_up_grad = lax.psum_scatter(
        jnp.einsum(
            "rd,rf->df", normed_slice, gate_up_rows, preferred_element_type=jnp.float32
        ).astype(jnp.bfloat16),
        "fsdp",
        scatter_dimension=0,
        tiled=True,
    )
    down_grad = lax.psum_scatter(
        jnp.einsum("rf,rd->fd", activated, d_branch, preferred_element_type=jnp.float32).astype(
            jnp.bfloat16
        ),
        "fsdp",
        scatter_dimension=0,
        tiled=True,
    )
    out_grad = lax.psum_scatter(
        jnp.einsum("rd,re->de", mixed, d_attended, preferred_element_type=jnp.float32).astype(
            jnp.bfloat16
        ),
        "fsdp",
        scatter_dimension=0,
        tiled=True,
    )
    d_mixed = (
        jnp.einsum("re,de->rd", d_attended, w_out_full, preferred_element_type=jnp.float32)
        .astype(jnp.bfloat16)
        .reshape(tokens, heads, head_dim)
    )

    def backward_group(packed):
        index, log_total = packed
        query_group, key_group, value_group, scores = group_scores(index)
        probs = jnp.exp(scores - log_total)
        d_group = lax.dynamic_slice_in_dim(d_mixed, index * group, group, 1)
        d_probs = jnp.einsum(
            "qgd,kgd->gqk", d_group, value_group, preferred_element_type=jnp.float32
        )
        d_scores = (probs * (d_probs - jnp.sum(d_probs * probs, axis=-1, keepdims=True))).astype(
            jnp.bfloat16
        )
        d_query = (
            jnp.einsum("gqk,kgd->qgd", d_scores, key_group, preferred_element_type=jnp.float32)
            * scale
        )
        d_key = (
            jnp.einsum("gqk,qgd->kgd", d_scores, query_group, preferred_element_type=jnp.float32)
            * scale
        )
        d_value = jnp.einsum(
            "gqk,qgd->kgd", probs.astype(jnp.bfloat16), d_group, preferred_element_type=jnp.float32
        )
        return (d_query, d_key, d_value)

    d_query_all, d_key_all, d_value_all = lax.map(backward_group, (jnp.arange(groups), log_totals))
    d_query = d_query_all.transpose(1, 0, 2, 3).reshape(tokens, heads, head_dim)
    d_key_full = d_key_all.transpose(1, 0, 2, 3).reshape(-1, width)
    d_value_full = d_value_all.transpose(1, 0, 2, 3).reshape(-1, width)
    d_key_own, d_value_own = (
        lax.psum_scatter(d_key_full, "seq", scatter_dimension=0, tiled=True),
        lax.psum_scatter(d_value_full, "seq", scatter_dimension=0, tiled=True),
    )
    d_projected = jnp.concatenate(
        [
            rotate(d_query, places, -1.0).reshape(tokens, width),
            rotate(d_key_own.reshape(tokens, heads, head_dim), places, -1.0).reshape(tokens, width),
            d_value_own,
        ],
        axis=1,
    ).astype(jnp.bfloat16)
    qkv_bias_term = jnp.sum(d_projected.astype(jnp.float32), axis=0)
    d_normed_one = jnp.einsum(
        "re,de->rd", d_projected, w_qkv_full, preferred_element_type=jnp.float32
    )
    gain_one_grad = jnp.sum(d_normed_one * centred_one, axis=0)
    bias_one_grad = jnp.sum(d_normed_one, axis=0)
    input_grad = (
        d_residual + norm_back(d_normed_one, centred_one, inverse_one, gain_one.astype(jnp.float32))
    ).astype(jnp.bfloat16)
    normed_slice = normed_one
    qkv_grad = lax.psum_scatter(
        jnp.einsum(
            "rd,re->de", normed_slice, d_projected, preferred_element_type=jnp.float32
        ).astype(jnp.bfloat16),
        "fsdp",
        scatter_dimension=0,
        tiled=True,
    )
    gain_one_part, bias_one_part, qkv_bias_part, gain_two_part, bias_two_part = (
        lax.psum_scatter(
            gain_one_grad.astype(jnp.bfloat16), "fsdp", scatter_dimension=0, tiled=True
        ).astype(jnp.float32),
        lax.psum_scatter(
            bias_one_grad.astype(jnp.bfloat16), "fsdp", scatter_dimension=0, tiled=True
        ).astype(jnp.float32),
        lax.psum_scatter(
            qkv_bias_term.astype(jnp.bfloat16), "fsdp", scatter_dimension=0, tiled=True
        ).astype(jnp.float32),
        lax.psum_scatter(
            gain_two_grad.astype(jnp.bfloat16), "fsdp", scatter_dimension=0, tiled=True
        ).astype(jnp.float32),
        lax.psum_scatter(
            bias_two_grad.astype(jnp.bfloat16), "fsdp", scatter_dimension=0, tiled=True
        ).astype(jnp.float32),
    )
    summed = (
        lax.psum(gain_one_part.astype(jnp.bfloat16), "seq").astype(jnp.float32),
        lax.psum(bias_one_part.astype(jnp.bfloat16), "seq").astype(jnp.float32),
        lax.psum(qkv_grad, "seq").astype(jnp.float32),
        lax.psum(qkv_bias_part.astype(jnp.bfloat16), "seq").astype(jnp.float32),
        lax.psum(out_grad, "seq").astype(jnp.float32),
        lax.psum(gain_two_part.astype(jnp.bfloat16), "seq").astype(jnp.float32),
        lax.psum(bias_two_part.astype(jnp.bfloat16), "seq").astype(jnp.float32),
        lax.psum(gate_up_grad, "seq").astype(jnp.float32),
        lax.psum(down_grad, "seq").astype(jnp.float32),
    )
    gate_up_total = summed[7]
    return (
        block_out[None],
        input_grad[None],
        summed[0],
        summed[1],
        summed[2],
        summed[3],
        summed[4],
        summed[5],
        summed[6],
        gate_up_total[:, :ffn_width],
        gate_up_total[:, ffn_width:],
        summed[8],
    )


def solution(mesh):
    return jax.shard_map(
        body,
        mesh=mesh,
        in_specs=(
            P("fsdp", "seq", None),
            P("fsdp", "seq", None),
            P(),
            P("fsdp"),
            P("fsdp"),
            P("fsdp", None),
            P("fsdp"),
            P("fsdp", None),
            P("fsdp"),
            P("fsdp"),
            P("fsdp", None),
            P("fsdp", None),
            P("fsdp", None),
        ),
        out_specs=(
            P("fsdp", "seq", None),
            P("fsdp", "seq", None),
            P("fsdp"),
            P("fsdp"),
            P("fsdp", None),
            P("fsdp"),
            P("fsdp", None),
            P("fsdp"),
            P("fsdp"),
            P("fsdp", None),
            P("fsdp", None),
            P("fsdp", None),
        ),
        check_vma=False,
    )
```

profile of v0, /device:TPU:0, one launch (start us, length us, event | category | flops | bytes accessed | tf_op | source)
XLA Modules:
  0.0 2643.6 jit_solution(6911663697845199274)
XLA Ops:
  8.0 15.7 all-gather.2
  23.7 12.1 all-gather.1
  35.9 11.8 all-gather
  48.4 184.0 %all-gather.13.cloned.1.call-done = bf16[2048,6144]{1,0:T(8,128)(2,1)} async-done(((bf16[256,6144]{1,0:T(8,128)(2,1)}), bf16[2048,6144]{1,0:T(8,128)(2,1)}) %all-gather.13.cloned.1.call-update) | async-done | bytes 25165840 | tf_op jit(solution)/shard_map/all_gather | solution.py:77
  232.4 11.8 convolution_add_fusion
  249.1 3.9 fusion.75
  253.0 3.1 copy.43
  264.7 8.7 all-gather.4
  273.4 10.2 all-gather.3
  285.4 13.6 all-gather.15.cloned.1.call-done
  298.9 6.6 copy.42
  305.5 48.3 %all-gather.17.cloned.1.call-done = bf16[1024,2048]{0,1:T(8,128)(2,1)} async-done(((bf16[256,2048]{0,1:T(8,128)(2,1)}), bf16[1024,2048]{0,1:T(8,128)(2,1)}) %all-gather.17.cloned.1.call-update) | async-done | bytes 4194320 | tf_op jit(solution)/shard_map/all_gather | solution.py:96
  353.8 39.9 %while.30 = (s32[]{:T(128)}, bf16[4,256,8,64]{1,3,2,0:T(8,128)(2,1)S(1)}, f32[4,8,256,1]{2,1,3,0:T(8,128)S(1)}, s32[4]{0:T(128)S(1)}, bf16[1024,32,64]{0,2,1:T(8...) while((s32[]{:T(128)}, ...), condition=%wide.region_5.6_spmd.clone.clone, body=%wide.region_2.5_spmd.clone.sunk.clone | while | flops 560199680 | bytes 29169844 | solution.py:123
  355.3 2.8 fusion.129
  360.3 3.4 fusion.130
  365.2 2.9 fusion.129
  370.3 3.4 fusion.130
  375.3 2.8 fusion.129
  380.3 3.4 fusion.130
  385.2 2.8 fusion.129
  390.3 3.4 fusion.130
  393.8 43.6 %all-gather.19.cloned.1.call-done = bf16[2048,2048]{1,0:T(8,128)(2,1)} async-done(((bf16[256,2048]{1,0:T(8,128)(2,1)}), bf16[2048,2048]{1,0:T(8,128)(2,1)}) %all-gather.19.cloned.1.call-update) | async-done | bytes 8388624 | tf_op jit(solution)/shard_map/all_gather | solution.py:79
  437.3 6.1 fusion.77
  443.9 196.1 %all-gather.21.cloned.1.call-done = bf16[2048,5632]{1,0:T(8,128)(2,1)} async-done(((bf16[256,5632]{1,0:T(8,128)(2,1)}), bf16[2048,5632]{1,0:T(8,128)(2,1)}) %all-gather.21.cloned.1.call-update) | async-done | bytes 23068688 | tf_op jit(solution)/shard_map/all_gather | solution.py:129
  640.0 15.1 fusion.79
  655.1 187.3 %all-gather.23.cloned.1.call-done = bf16[2048,5632]{1,0:T(8,128)(2,1)} async-done(((bf16[256,5632]{1,0:T(8,128)(2,1)}), bf16[2048,5632]{1,0:T(8,128)(2,1)}) %all-gather.23.cloned.1.call-update) | async-done | bytes 23068688 | tf_op jit(solution)/shard_map/all_gather | solution.py:130
  842.4 14.9 fusion.78
  857.3 187.6 %all-gather.25.cloned.1.call-done = bf16[5632,2048]{1,0:T(8,128)(2,1)} async-done(((bf16[704,2048]{1,0:T(8,128)(2,1)}), bf16[5632,2048]{1,0:T(8,128)(2,1)}) %all-gather.25.cloned.1.call-update) | async-done | bytes 23068688 | tf_op jit(solution)/shard_map/all_gather | solution.py:131
  1044.9 26.2 multiply_convert_fusion.1
  1071.0 12.5 fusion.80
  1083.5 13.9 multiply_reduce_fusion.1
  1101.3 5.8 convolution_convert_fusion.4
  1107.7 80.1 %while.31 = (s32[]{:T(128)}, f32[4,256,8,64]{1,3,2,0:T(8,128)}, f32[4,1024,8,64]{1,3,2,0:T(8,128)}, f32[4,1024,8,64]{1,3,2,0:T(8,128)}, s32[4]{0:T(128)S(1)}, /*...) while((s32[]{:T(128)}, f32[4,256,8,64]{1,3,2,0:T(8,128)}, ...), condition=%wide.region_12.13_spmd.clone.clone, body=%wide.region_10.12_spmd.clone.sunk.clone | while | flops 1374550016 | bytes 72940760 | solution.py:225
  1111.9 4.5 multiply_reduce_fusion.9
  1118.7 3.4 fusion.140
  1124.3 3.6 bitcast_dynamic-update-slice_fusion.11
  1131.9 4.5 multiply_reduce_fusion.9
  1138.7 3.4 fusion.140
  1144.3 3.5 bitcast_dynamic-update-slice_fusion.11
  1151.9 4.5 multiply_reduce_fusion.9
  1158.7 3.4 fusion.140
  1164.3 3.5 bitcast_dynamic-update-slice_fusion.11
  1171.8 4.5 multiply_reduce_fusion.9
  1178.6 3.4 fusion.140
  1184.2 3.5 bitcast_dynamic-update-slice_fusion.11
  1189.7 5.6 convolution_convert_fusion.3
  1197.1 12.6 convolution_convert_fusion.1
  1211.5 60.9 %reduce-scatter.9.cloned.1.call-done = f32[256,2048]{0,1:T(8,128)} async-done(((f32[1024,2048]{0,1:T(8,128)}), f32[256,2048]{0,1:T(8,128)}) %reduce-scatter.9.cloned.1.call-update) | async-done | bytes 2097168 | tf_op jit(solution)/shard_map/reduce_scatter | solution.py:230
  1274.0 87.9 %reduce-scatter.11.cloned.1.call-done = f32[256,2048]{0,1:T(8,128)} async-done(((f32[1024,2048]{0,1:T(8,128)}), f32[256,2048]{0,1:T(8,128)}) %reduce-scatter.11.cloned.1.call-update) | async-done | bytes 2097168 | tf_op jit(solution)/shard_map/reduce_scatter | solution.py:231
  1366.9 15.0 convolution_convert_fusion.2
  1383.6 21.3 convolution_convert_fusion
  1404.9 48.7 %reduce-scatter.15.cloned.1.call-done = bf16[256,2048]{1,0:T(8,128)(2,1)} async-done(((bf16[2048,2048]{1,0:T(8,128)(2,1)}), bf16[256,2048]{1,0:T(8,128)(2,1)}) %reduce-scatter.15.cloned.1.call-update) | async-done | bytes 1048592 | tf_op jit(solution)/shard_map/reduce_scatter | solution.py:187
  1453.6 228.2 %reduce-scatter.17.cloned.1.call-done = bf16[704,2048]{1,0:T(8,128)(2,1)} async-done(((bf16[5632,2048]{1,0:T(8,128)(2,1)}), bf16[704,2048]{1,0:T(8,128)(2,1)}) %reduce-scatter.17.cloned.1.call-update) | async-done | bytes 2883600 | tf_op jit(solution)/shard_map/reduce_scatter | solution.py:179
  1681.8 247.8 %reduce-scatter.13.cloned.1.call-done = bf16[256,6144]{1,0:T(8,128)(2,1)} async-done(((bf16[2048,6144]{1,0:T(8,128)(2,1)}), bf16[256,6144]{1,0:T(8,128)(2,1)}) %reduce-scatter.13.cloned.1.call-update) | async-done | bytes 3145744 | tf_op jit(solution)/shard_map/reduce_scatter | solution.py:251
  1929.6 444.5 %reduce-scatter.19.cloned.1.call-done = bf16[256,11264]{1,0:T(8,128)(2,1)} async-done(((bf16[2048,11264]{1,0:T(8,128)(2,1)}), bf16[256,11264]{1,0:T(8,128)(2,1)}) %reduce-scatter.19.cloned.1.call-update) | async-done | bytes 5767184
  2376.7 13.8 fusion.53
  2391.5 14.0 fusion.61
  2405.5 26.0 all-reduce.6
  2431.9 10.5 all-reduce.7
  2445.3 3.5 fusion.63
  2448.8 171.4 %all-reduce.11.cloned.1.call-done = (bf16[256,6144]{1,0:T(8,128)(2,1)}, bf16[256,2048]{1,0:T(8,128)(2,1)}, bf16[256,11264]{1,0:T(8,128)(2,1)}, bf16[704,2048]{1,0:T(8,128)(2,1)}) async-done(((bf16[256,6144]{1,0:T(8,128)(2,1)}, bf16[256,2048]{1,0:T(8,128)(2,1)}, bf16[256,11264]{1,0:T(8,128)(2,1)}, bf16[704,2048]{1,0:T(8,128)(2,1)}), (bf16[256,6144]{1,0:T(8,128)(2,1)}, bf16[256,2048]{1,0:T(8,128)(2,1)}, ...) | async-done | bytes 12845072 | tf_op jit(solution)/shard_map/psum | solution.py:279
  2620.3 5.5 convert_element_type.180
  2627.3 5.9 fusion.76
  2633.3 3.3 convert_element_type.191
  (235 shorter events, 85.2 us)
Async XLA Ops:
  7.2 16.5 copy-start.45
  7.2 28.7 %copy-start.46 = (bf16[256]{0:T(256)(128)(2,1)S(1)}, bf16[256]{0:T(256)(128)(2,1)}, u32[]{:S(2)}) copy-start(bf16[256]{0:T(256)(128)(2,1)} %param.20) | copy-start | bytes 1540
  7.2 40.5 %copy-start.2 = (bf16[1,256,2048]{2,1,0:T(8,128)(2,1)S(1)}, bf16[1,256,2048]{2,1,0:T(8,128)(2,1)}, u32[]{:S(2)}) copy-start(bf16[1,256,2048]{2,1,0:T(8,128)(2,1)} %param.17) | copy-start | bytes 3145732
  7.2 225.2 %all-gather.13.cloned.1.call-start = ((), (), s32[]{:S(2)}) async-start(), calls=%async_computation.6 | async-start | bytes 28311552 | tf_op jit(solution)/shard_map/all_gather | solution.py:77
  8.0 291.0 %all-gather.15.cloned.1.call-start = ((), (), s32[]{:S(2)}) async-start(), calls=%async_computation.7 | async-start | bytes 5242880 | tf_op jit(solution)/shard_map/all_gather | solution.py:97
  35.9 208.3 %copy-start.26 = (f32[8,1,256]{2,1,0:T(1,128)}, f32[8,1,256]{2,1,0:T(1,128)S(1)}, u32[]{:S(2)}) copy-start(f32[8,1,256]{2,1,0:T(1,128)S(1)} %convert_element_type.193) | copy-start | bytes 24580
  47.7 196.5 %copy-start.22 = (f32[8,1,256]{2,1,0:T(1,128)}, f32[8,1,256]{2,1,0:T(1,128)S(1)}, u32[]{:S(2)}) copy-start(f32[8,1,256]{2,1,0:T(1,128)S(1)} %convert_element_type.192) | copy-start | bytes 24580
  47.9 196.3 %copy-start.34 = (f32[256]{0:T(256)}, f32[256]{0:T(256)S(1)}, u32[]{:S(2)}) copy-start(f32[256]{0:T(256)S(1)} %broadcast_multiply_fusion.7) | copy-start | bytes 3076
  48.4 195.8 %copy-start.36 = (f32[256]{0:T(256)}, f32[256]{0:T(256)S(1)}, u32[]{:S(2)}) copy-start(f32[256]{0:T(256)S(1)} %add_rsqrt_fusion.1) | copy-start | bytes 3076
  244.2 2.7 copy-start.17
  246.9 1.2 copy-start.43
  248.1 105.7 %all-gather.17.cloned.1.call-start = ((), (), s32[]{:S(2)}) async-start(), calls=%async_computation.8 | async-start | bytes 5242880 | tf_op jit(solution)/shard_map/all_gather | solution.py:96
  249.1 10.4 copy-start.38
  261.9 175.4 %all-gather.19.cloned.1.call-start = ((), (), s32[]{:S(2)}) async-start(), calls=%async_computation.9 | async-start | bytes 9437184 | tf_op jit(solution)/shard_map/all_gather | solution.py:79
  262.5 377.5 %all-gather.21.cloned.1.call-start = ((), (), s32[]{:S(2)}) async-start(), calls=%async_computation.10 | async-start | bytes 25952256 | tf_op jit(solution)/shard_map/all_gather | solution.py:129
  263.1 1.5 copy-start.47
  263.1 10.2 copy-start.48
  263.1 579.2 %all-gather.23.cloned.1.call-start = ((), (), s32[]{:S(2)}) async-start(), calls=%async_computation.11 | async-start | bytes 25952256 | tf_op jit(solution)/shard_map/all_gather | solution.py:130
  263.7 781.2 %all-gather.25.cloned.1.call-start = ((), (), s32[]{:S(2)}) async-start(), calls=%async_computation.12 | async-start | bytes 25952256 | tf_op jit(solution)/shard_map/all_gather | solution.py:131
  264.5 1008.0 %reduce-scatter.9.cloned.1.call-start = ((), (), s32[]{:S(2)}) async-start(), calls=%async_computation.13 | async-start | bytes 10485760 | tf_op jit(solution)/shard_map/reduce_scatter | solution.py:230
  273.3 569.0 %copy-start.28 = (f32[8,1,256]{2,1,0:T(1,128)}, f32[8,1,256]{2,1,0:T(1,128)S(1)}, u32[]{:S(2)}) copy-start(f32[8,1,256]{2,1,0:T(1,128)S(1)} %convert_element_type.196) | copy-start | bytes 24580
  283.5 813.9 %copy-start.24 = (f32[8,1,256]{2,1,0:T(1,128)}, f32[8,1,256]{2,1,0:T(1,128)S(1)}, u32[]{:S(2)}) copy-start(f32[8,1,256]{2,1,0:T(1,128)S(1)} %convert_element_type.195) | copy-start | bytes 24580
  393.7 43.6 %copy-start.4 = (bf16[256,32,64]{0,2,1:T(8,128)(2,1)}, bf16[256,32,64]{0,2,1:T(8,128)(2,1)S(1)}, u32[]{:S(2)}) copy-start(bf16[256,32,64]{0,2,1:T(8,128)(2,1)S(1)} %get-tuple-element.592) | copy-start | bytes 3145732
  393.7 43.6 %copy-start.9 = (bf16[4,256,8,64]{1,3,2,0:T(8,128)(2,1)}, bf16[4,256,8,64]{1,3,2,0:T(8,128)(2,1)S(1)}, u32[]{:S(2)}) copy-start(bf16[4,256,8,64]{1,3,2,0:T(8,128)(2,1)S(1)} %get-tuple-element.114) | copy-start | bytes 3145732
  443.5 654.0 %copy-start = (f32[256,2048]{1,0:T(8,128)}, f32[256,2048]{1,0:T(8,128)S(1)}, u32[]{:S(2)}) copy-start(f32[256,2048]{1,0:T(8,128)S(1)} %get-tuple-element.285) | copy-start | bytes 6291460
  443.5 653.9 %copy-start.30 = (f32[256]{0:T(256)}, f32[256]{0:T(256)S(1)}, u32[]{:S(2)}) copy-start(f32[256]{0:T(256)S(1)} %broadcast_multiply_fusion.6) | copy-start | bytes 3076
  443.9 653.6 %copy-start.32 = (f32[256]{0:T(256)}, f32[256]{0:T(256)S(1)}, u32[]{:S(2)}) copy-start(f32[256]{0:T(256)S(1)} %add_rsqrt_fusion) | copy-start | bytes 3076
  655.1 389.8 %copy-start.19 = (bf16[1,256,2048]{2,1,0:T(8,128)(2,1)S(1)}, bf16[1,256,2048]{2,1,0:T(8,128)(2,1)}, u32[]{:S(2)}) copy-start(bf16[1,256,2048]{2,1,0:T(8,128)(2,1)} %param.18) | copy-start | bytes 3145732
  1099.9 1.3 copy-start.6
  1101.3 6.4 copy-start.5
  1187.8 174.1 %reduce-scatter.11.cloned.1.call-start = ((), (), s32[]{:S(2)}) async-start(), calls=%async_computation.14 | async-start | bytes 10485760 | tf_op jit(solution)/shard_map/reduce_scatter | solution.py:231
  1187.9 1.6 copy-start.7
  1187.9 1.8 copy-start.10
  1188.5 265.0 %reduce-scatter.15.cloned.1.call-start = ((), (), s32[]{:S(2)}) async-start(), calls=%async_computation.16 | async-start | bytes 9437184 | tf_op jit(solution)/shard_map/reduce_scatter | solution.py:187
  1195.3 1.8 copy-start.18
  1195.4 486.4 %reduce-scatter.17.cloned.1.call-start = ((), (), s32[]{:S(2)}) async-start(), calls=%async_computation.17 | async-start | bytes 25952256 | tf_op jit(solution)/shard_map/reduce_scatter | solution.py:179
  1209.7 719.8 %reduce-scatter.13.cloned.1.call-start = ((), (), s32[]{:S(2)}) async-start(), calls=%async_computation.15 | async-start | bytes 28311552 | tf_op jit(solution)/shard_map/reduce_scatter | solution.py:251
  1209.8 153.9 %copy-start.39 = (f32[256,8]{0,1:T(8,128)S(1)}, f32[256,8]{0,1:T(8,128)}, u32[]{:S(2)}) copy-start(f32[256,8]{0,1:T(8,128)} %copy-done.38) | copy-start | bytes 24580
  1209.8 153.9 %copy-start.40 = (f32[256,8]{0,1:T(8,128)S(1)}, f32[256,8]{0,1:T(8,128)}, u32[]{:S(2)}) copy-start(f32[256,8]{0,1:T(8,128)} %get-tuple-element.279) | copy-start | bytes 24580
  1363.6 2.1 copy-start.11
  1363.6 3.3 copy-start.3
  1363.6 3.3 copy-start.23
  1363.6 3.3 copy-start.27
  1363.6 3.2 copy-start.35
  1363.6 3.2 copy-start.37
  1365.5 1.0 copy-start.13
  1365.7 1.2 copy-start.15
  1381.9 1.6 copy-start.1
  1381.9 1.6 copy-start.25
  1381.9 1.6 copy-start.29
  1381.9 1.6 copy-start.31
  1382.0 1.6 copy-start.33
  1382.0 992.1 %reduce-scatter.19.cloned.1.call-start = ((), (), s32[]{:S(2)}) async-start(), calls=%async_computation.18 | async-start | bytes 51904512
  1404.9 1215.4 %all-reduce.11.cloned.1.call-start = ((), (), s32[]{:S(2)}) async-start(), calls=%async_computation.19 | async-start | bytes 25690112 | tf_op jit(solution)/shard_map/psum | solution.py:279
  2376.6 13.8 copy-start.12
  2376.7 13.8 copy-start.14
  2376.7 13.8 copy-start.16
  2391.5 14.0 copy-start.41
  2391.5 14.0 copy-start.42
  2391.5 53.8 %copy-start.8 = (f32[256,2048]{1,0:T(8,128)S(1)}, f32[256,2048]{1,0:T(8,128)}, u32[]{:S(2)}) copy-start(f32[256,2048]{1,0:T(8,128)} %copy-done.6) | copy-start | bytes 6291460
  2620.3 7.1 slice-start
  2620.3 5.5 copy-start.21
  2620.3 7.1 slice-start.1
  2627.3 5.9 copy-start.20
  (2 other events, 1.5 us)
Sparse Core Ops, SparseCore 0:
  9.7 222.6 all-gather.12
  248.2 50.6 all-gather.14
  301.3 52.4 all-gather.16
  355.3 82.0 all-gather.18
  438.8 201.1 all-gather.20
  641.5 200.8 all-gather.22
  844.0 200.8 all-gather.24
  1187.9 84.4 reduce-scatter.8
  1275.5 86.3 reduce-scatter.10
  1364.0 89.5 reduce-scatter.14
  1456.0 225.7 reduce-scatter.16
  1684.0 245.5 reduce-scatter.12
  1932.0 442.1 reduce-scatter.18
  2377.9 242.2 all-reduce.10
where the time goes:
time: 2650 us; the launch traced here: 2640 us
  waiting for transfers between devices  2150 us (81%)
  matrix products  278 us (10%)
  blocking collectives  94.9 us (4%)
  other arithmetic  48.4 us (2%)
  local copies, waits for them, and re-layouts  45.4 us (2%)
    unnamed x15, waiting for transfers between devices  448 us
    reduce_scatter x1, waiting for transfers between devices, body(): lax.psum_scatter(jnp.einsum('rd,re->de', normed_slice, d_projected, prefe...  248 us
    reduce_scatter x1, waiting for transfers between devices, body(): lax.psum_scatter(jnp.einsum('rf,rd->fd', activated, d_branch, preferred_e...  228 us
    all_gather x1, waiting for transfers between devices, body(): lax.all_gather(gate_weight, 'fsdp', axis=0, tiled=True)  196 us
    all_gather x1, waiting for transfers between devices, body(): lax.all_gather(down_weight, 'fsdp', axis=0, tiled=True)  188 us
    all_gather x1, waiting for transfers between devices, body(): lax.all_gather(up_weight, 'fsdp', axis=0, tiled=True)  187 us
    all_gather x1, waiting for transfers between devices, body(): lax.all_gather(qkv_weight, 'fsdp', axis=0, tiled=True)  184 us
    psum x1, waiting for transfers between devices, body(): lax.psum(qkv_grad, 'seq').astype(jnp.float32)  171 us
  transfers between devices with their start and end apart: 14, of which 14 were waited for; matrix products, arithmetic and copies ran while one was open for 7% of the time, Pallas kernels for 0%

commit v1 on v0

--- a/solution.py
+++ b/solution.py
@@ -127,7 +127,9 @@
         lax.all_gather(second_gain, "fsdp", axis=0, tiled=True),
         lax.all_gather(second_bias, "fsdp", axis=0, tiled=True),
         lax.all_gather(gate_weight, "fsdp", axis=0, tiled=True),
-        lax.all_gather(up_weight, "fsdp", axis=0, tiled=True),
+        jnp.concatenate(
+            lax.all_to_all(jnp.stack([up_weight] * lax.axis_size("fsdp")), "fsdp", 0, 0), axis=0
+        ),
         lax.all_gather(down_weight, "fsdp", axis=0, tiled=True),
     )
     centred_two, inverse_two = normalize(residual)

time: 2650 us -> 2990 us (1.13)
  blocking collectives: 94.9 us -> 942 us
  waiting for transfers between devices: 2150 us -> 1630 us
    all_gather x1, blocking collectives: 8.65 us -> 597 us  [body(): lax.all_gather(second_bias, 'fsdp', axis=0, tiled=True)]
    all_gather x1, blocking collectives: 10.2 us -> 269 us  [body(): lax.all_gather(second_gain, 'fsdp', axis=0, tiled=True)]
    all_gather x1, waiting for transfers between devices: 196 us -> 0.01 us  [body(): lax.all_gather(gate_weight, 'fsdp', axis=0, tiled=True)]
    all_gather x1, waiting for transfers between devices: 188 us -> 0.01 us  [body(): lax.all_gather(down_weight, 'fsdp', axis=0, tiled=True)]
    all_gather x1, waiting for transfers between devices: 48.3 us -> 0.01 us  [body(): lax.all_gather(key_rot.reshape(tokens, width), 'seq', axis=0, tiled=True)]
    all_gather x1, waiting for transfers between devices: 43.6 us -> 0.02 us  [body(): lax.all_gather(out_weight, 'fsdp', axis=0, tiled=True)]
    all_gather x1, waiting for transfers between devices: 187 us -> 151 us  [body(): lax.all_gather(up_weight, 'fsdp', axis=0, tiled=True)]
  transfers between devices with their start and end apart: 14 -> 15, of which waited for: 14 -> 9; matrix products, arithmetic and copies ran while one was open for 7% -> 8% of each run, Pallas kernels for 0% -> 0%
where the time goes in v1:
time: 2990 us; the launch traced here: 2980 us
  waiting for transfers between devices  1630 us (55%)
  blocking collectives  942 us (32%)
  matrix products  278 us (9%)
  local copies, waits for them, and re-layouts  55.8 us (2%)
  other arithmetic  48.5 us (2%)
    all_gather x1, blocking collectives, body(): lax.all_gather(second_bias, 'fsdp', axis=0, tiled=True)  597 us
    unnamed x15, waiting for transfers between devices  448 us
    all_gather x1, blocking collectives, body(): lax.all_gather(second_gain, 'fsdp', axis=0, tiled=True)  269 us
    reduce_scatter x1, waiting for transfers between devices, body(): lax.psum_scatter(jnp.einsum('rd,re->de', normed_slice, d_projected, prefe...  248 us
    reduce_scatter x1, waiting for transfers between devices, body(): lax.psum_scatter(jnp.einsum('rf,rd->fd', activated, d_branch, preferred_e...  228 us
    all_gather x1, waiting for transfers between devices, body(): lax.all_gather(qkv_weight, 'fsdp', axis=0, tiled=True)  184 us
    psum x1, waiting for transfers between devices, body(): lax.psum(qkv_grad, 'seq').astype(jnp.float32)  171 us
    all_gather x1, waiting for transfers between devices, body(): lax.all_gather(up_weight, 'fsdp', axis=0, tiled=True)  151 us
  transfers between devices with their start and end apart: 15, of which 9 were waited for; matrix products, arithmetic and copies ran while one was open for 8% of the time, Pallas kernels for 0%

profile of v1, /device:TPU:0, one launch (start us, length us, event | category | flops | bytes accessed | tf_op | source)
XLA Modules:
  0.0 2981.7 jit_solution(960024673413253234)
XLA Ops:
  8.0 15.7 all-gather.2
  23.7 12.1 all-gather.1
  35.9 11.8 all-gather
  48.4 184.0 %all-gather.13.cloned.1.call-done = bf16[2048,6144]{1,0:T(8,128)(2,1)} async-done(((bf16[256,6144]{1,0:T(8,128)(2,1)}), bf16[2048,6144]{1,0:T(8,128)(2,1)}) %all-gather.13.cloned.1.call-update) | async-done | bytes 25165840 | tf_op jit(solution)/shard_map/all_gather | solution.py:77
  232.4 11.8 convolution_add_fusion
  244.2 2.7 copy-done.17
  249.1 3.9 fusion.75
  253.0 3.1 copy.43
  263.7 9.0 stack.2
  272.8 6.4 all-to-all-start
  280.1 596.9 %all-gather.4 = bf16[8,1,256]{2,1,0:T(2,128)(2,1)S(1)} all-gather(bf16[1,1,256]{2,1,0:T(2,128)(2,1)S(1)} %reshape.295), channel_id=1, replica_groups=mesh['seq'=4,'fsdp'=8] {'fsdp'}, dimensions={0}, use_global_device_ids=true | all-gather | bytes 4608 | tf_op jit(solution)/shard_map/all_gather | solution.py:128
  877.1 268.7 %all-gather.3 = bf16[8,1,256]{2,1,0:T(2,128)(2,1)S(1)} all-gather(bf16[1,1,256]{2,1,0:T(2,128)(2,1)S(1)} %reshape.293), channel_id=1, replica_groups=mesh['seq'=4,'fsdp'=8] {'fsdp'}, dimensions={0}, use_global_device_ids=true | all-gather | bytes 4608 | tf_op jit(solution)/shard_map/all_gather | solution.py:127
  1147.6 6.6 copy.42
  1154.3 39.8 %while.30 = (s32[]{:T(128)}, bf16[4,256,8,64]{1,3,2,0:T(8,128)(2,1)S(1)}, f32[4,8,256,1]{2,1,3,0:T(8,128)S(1)}, s32[4]{0:T(128)S(1)}, bf16[1024,32,64]{0,2,1:T(8...) while((s32[]{:T(128)}, ...), condition=%wide.region_5.6_spmd.clone.clone, body=%wide.region_2.5_spmd.clone.sunk.clone | while | flops 560199680 | bytes 29169844 | solution.py:123
  1155.7 2.8 fusion.129
  1160.8 3.4 fusion.130
  1165.7 2.9 fusion.129
  1170.8 3.4 fusion.130
  1175.7 2.8 fusion.129
  1180.7 3.4 fusion.130
  1185.6 2.8 fusion.129
  1190.7 3.4 fusion.130
  1195.4 6.1 fusion.77
  1202.0 13.8 fusion.78
  1215.8 14.1 fusion.79
  1229.9 28.0 multiply_convert_fusion.1
  1257.9 12.7 fusion.80
  1270.6 151.0 %all-gather.25.cloned.1.call-done = bf16[2048,5632]{1,0:T(8,128)(2,1)} async-done(((bf16[256,5632]{1,0:T(8,128)(2,1)}), bf16[2048,5632]{1,0:T(8,128)(2,1)}) %all-gather.25.cloned.1.call-update) | async-done | bytes 23068688 | tf_op jit(solution)/shard_map/all_gather | solution.py:154
  1421.6 13.8 multiply_reduce_fusion.1
  1439.2 5.8 convolution_convert_fusion.4
  1445.6 80.3 %while.31 = (s32[]{:T(128)}, f32[4,256,8,64]{1,3,2,0:T(8,128)}, f32[4,1024,8,64]{1,3,2,0:T(8,128)}, f32[4,1024,8,64]{1,3,2,0:T(8,128)}, s32[4]{0:T(128)S(1)}, /*...) while((s32[]{:T(128)}, f32[4,256,8,64]{1,3,2,0:T(8,128)}, ...), condition=%wide.region_12.13_spmd.clone.clone, body=%wide.region_10.12_spmd.clone.sunk.clone | while | flops 1374550016 | bytes 72940760 | solution.py:227
  1447.0 2.5 fusion.139
  1449.8 4.5 multiply_reduce_fusion.9
  1456.6 3.4 fusion.140
  1462.2 3.5 bitcast_dynamic-update-slice_fusion.11
  1469.8 4.5 multiply_reduce_fusion.9
  1476.6 3.4 fusion.140
  1482.2 3.6 bitcast_dynamic-update-slice_fusion.11
  1487.0 2.5 fusion.139
  1489.7 4.5 multiply_reduce_fusion.9
  1496.6 3.5 fusion.140
  1502.2 3.5 bitcast_dynamic-update-slice_fusion.11
  1509.8 4.5 multiply_reduce_fusion.9
  1516.6 3.5 fusion.140
  1522.3 3.6 bitcast_dynamic-update-slice_fusion.11
  1527.8 5.6 convolution_convert_fusion.3
  1535.3 12.6 convolution_convert_fusion.1
  1549.6 60.9 %reduce-scatter.9.cloned.1.call-done = f32[256,2048]{0,1:T(8,128)} async-done(((f32[1024,2048]{0,1:T(8,128)}), f32[256,2048]{0,1:T(8,128)}) %reduce-scatter.9.cloned.1.call-update) | async-done | bytes 2097168 | tf_op jit(solution)/shard_map/reduce_scatter | solution.py:232
  1612.1 87.9 %reduce-scatter.11.cloned.1.call-done = f32[256,2048]{0,1:T(8,128)} async-done(((f32[1024,2048]{0,1:T(8,128)}), f32[256,2048]{0,1:T(8,128)}) %reduce-scatter.11.cloned.1.call-update) | async-done | bytes 2097168 | tf_op jit(solution)/shard_map/reduce_scatter | solution.py:233
  1705.0 15.0 convolution_convert_fusion.2
  1721.6 21.3 convolution_convert_fusion
  1743.0 48.7 %reduce-scatter.15.cloned.1.call-done = bf16[256,2048]{1,0:T(8,128)(2,1)} async-done(((bf16[2048,2048]{1,0:T(8,128)(2,1)}), bf16[256,2048]{1,0:T(8,128)(2,1)}) %reduce-scatter.15.cloned.1.call-update) | async-done | bytes 1048592 | tf_op jit(solution)/shard_map/reduce_scatter | solution.py:189
  1791.7 228.2 %reduce-scatter.17.cloned.1.call-done = bf16[704,2048]{1,0:T(8,128)(2,1)} async-done(((bf16[5632,2048]{1,0:T(8,128)(2,1)}), bf16[704,2048]{1,0:T(8,128)(2,1)}) %reduce-scatter.17.cloned.1.call-update) | async-done | bytes 2883600 | tf_op jit(solution)/shard_map/reduce_scatter | solution.py:181
  2019.9 247.8 %reduce-scatter.13.cloned.1.call-done = bf16[256,6144]{1,0:T(8,128)(2,1)} async-done(((bf16[2048,6144]{1,0:T(8,128)(2,1)}), bf16[256,6144]{1,0:T(8,128)(2,1)}) %reduce-scatter.13.cloned.1.call-update) | async-done | bytes 3145744 | tf_op jit(solution)/shard_map/reduce_scatter | solution.py:253
  2267.7 444.5 %reduce-scatter.19.cloned.1.call-done = bf16[256,11264]{1,0:T(8,128)(2,1)} async-done(((bf16[2048,11264]{1,0:T(8,128)(2,1)}), bf16[256,11264]{1,0:T(8,128)(2,1)}) %reduce-scatter.19.cloned.1.call-update) | async-done | bytes 5767184
  2714.8 13.8 fusion.53
  2729.6 14.0 fusion.61
  2743.6 26.0 all-reduce.6
  2770.0 10.6 all-reduce.7
  2783.5 3.5 fusion.63
  2787.0 171.4 %all-reduce.11.cloned.1.call-done = (bf16[256,6144]{1,0:T(8,128)(2,1)}, bf16[256,2048]{1,0:T(8,128)(2,1)}, bf16[256,11264]{1,0:T(8,128)(2,1)}, bf16[704,2048]{1,0:T(8,128)(2,1)}) async-done(((bf16[256,6144]{1,0:T(8,128)(2,1)}, bf16[256,2048]{1,0:T(8,128)(2,1)}, bf16[256,11264]{1,0:T(8,128)(2,1)}, bf16[704,2048]{1,0:T(8,128)(2,1)}), (bf16[256,6144]{1,0:T(8,128)(2,1)}, bf16[256,2048]{1,0:T(8,128)(2,1)}, ...) | async-done | bytes 12845072 | tf_op jit(solution)/shard_map/psum | solution.py:281
  2958.4 5.5 convert_element_type.180
  2965.4 5.9 fusion.76
  2971.4 3.3 convert_element_type.191
  (238 shorter events, 78.8 us)
Async XLA Ops:
  7.2 16.5 copy-start.45
  7.2 28.7 copy-start.46
  7.2 40.5 %copy-start.2 = (bf16[1,256,2048]{2,1,0:T(8,128)(2,1)S(1)}, bf16[1,256,2048]{2,1,0:T(8,128)(2,1)}, u32[]{:S(2)}) copy-start(bf16[1,256,2048]{2,1,0:T(8,128)(2,1)} %param.17) | copy-start | bytes 3145732
  7.2 225.2 %all-gather.13.cloned.1.call-start = ((), (), s32[]{:S(2)}) async-start(), calls=%async_computation.7 | async-start | bytes 28311552 | tf_op jit(solution)/shard_map/all_gather | solution.py:77
  8.0 1139.7 %all-gather.15.cloned.1.call-start = ((), (), s32[]{:S(2)}) async-start(), calls=%async_computation.8 | async-start | bytes 5242880 | tf_op jit(solution)/shard_map/all_gather | solution.py:97
  35.9 208.3 %copy-start.26 = (f32[8,1,256]{2,1,0:T(1,128)}, f32[8,1,256]{2,1,0:T(1,128)S(1)}, u32[]{:S(2)}) copy-start(f32[8,1,256]{2,1,0:T(1,128)S(1)} %convert_element_type.193) | copy-start | bytes 24580
  47.7 196.5 %copy-start.22 = (f32[8,1,256]{2,1,0:T(1,128)}, f32[8,1,256]{2,1,0:T(1,128)S(1)}, u32[]{:S(2)}) copy-start(f32[8,1,256]{2,1,0:T(1,128)S(1)} %convert_element_type.192) | copy-start | bytes 24580
  47.9 196.3 %copy-start.34 = (f32[256]{0:T(256)}, f32[256]{0:T(256)S(1)}, u32[]{:S(2)}) copy-start(f32[256]{0:T(256)S(1)} %broadcast_multiply_fusion.7) | copy-start | bytes 3076
  48.4 195.8 %copy-start.36 = (f32[256]{0:T(256)}, f32[256]{0:T(256)S(1)}, u32[]{:S(2)}) copy-start(f32[256]{0:T(256)S(1)} %add_rsqrt_fusion.1) | copy-start | bytes 3076
  244.2 2.7 copy-start.17
  246.9 1.2 copy-start.43
  248.1 906.2 %all-gather.17.cloned.1.call-start = ((), (), s32[]{:S(2)}) async-start(), calls=%async_computation.9 | async-start | bytes 5242880 | tf_op jit(solution)/shard_map/all_gather | solution.py:96
  249.1 10.4 copy-start.38
  262.0 932.2 %all-gather.19.cloned.1.call-start = ((), (), s32[]{:S(2)}) async-start(), calls=%async_computation.10 | async-start | bytes 9437184 | tf_op jit(solution)/shard_map/all_gather | solution.py:79
  262.6 953.2 %all-gather.21.cloned.1.call-start = ((), (), s32[]{:S(2)}) async-start(), calls=%async_computation.11 | async-start | bytes 25952256 | tf_op jit(solution)/shard_map/all_gather | solution.py:129
  263.2 966.7 %all-gather.23.cloned.1.call-start = ((), (), s32[]{:S(2)}) async-start(), calls=%async_computation.12 | async-start | bytes 25952256 | tf_op jit(solution)/shard_map/all_gather | solution.py:133
  272.8 7.4 copy-start.47
  272.8 604.3 %copy-start.48 = (bf16[256]{0:T(256)(128)(2,1)S(1)}, bf16[256]{0:T(256)(128)(2,1)}, u32[]{:S(2)}) copy-start(bf16[256]{0:T(256)(128)(2,1)} %param.25) | copy-start | bytes 1540
  272.8 929.2 %all-to-all-start = ((bf16[8,256,5632]{2,1,0:T(8,128)(2,1)}), bf16[8,256,5632]{2,1,0:T(8,128)(2,1)}, u32[]{:S(2)}, u32[]{:S(2)}) async-start(bf16[8,256,5632]{2,1,0:T(8,128)(2,1)} %stack.2), calls=%async_computation | async-start | bytes 46137344 | tf_op jit(solution)/shard_map/all_to_all | solution.py:131
  279.2 1142.4 %all-gather.25.cloned.1.call-start = ((), (), s32[]{:S(2)}) async-start(), calls=%async_computation.13 | async-start | bytes 25952256 | tf_op jit(solution)/shard_map/all_gather | solution.py:154
  280.0 1330.6 %reduce-scatter.9.cloned.1.call-start = ((), (), s32[]{:S(2)}) async-start(), calls=%async_computation.14 | async-start | bytes 10485760 | tf_op jit(solution)/shard_map/reduce_scatter | solution.py:232
  877.0 338.7 %copy-start.28 = (f32[8,1,256]{2,1,0:T(1,128)}, f32[8,1,256]{2,1,0:T(1,128)S(1)}, u32[]{:S(2)}) copy-start(f32[8,1,256]{2,1,0:T(1,128)S(1)} %convert_element_type.196) | copy-start | bytes 24580
  1145.8 289.6 %copy-start.24 = (f32[8,1,256]{2,1,0:T(1,128)}, f32[8,1,256]{2,1,0:T(1,128)S(1)}, u32[]{:S(2)}) copy-start(f32[8,1,256]{2,1,0:T(1,128)S(1)} %convert_element_type.195) | copy-start | bytes 24580
  1194.1 1.3 copy-start.9
  1201.6 233.8 %copy-start = (f32[256,2048]{1,0:T(8,128)}, f32[256,2048]{1,0:T(8,128)S(1)}, u32[]{:S(2)}) copy-start(f32[256,2048]{1,0:T(8,128)S(1)} %get-tuple-element.285) | copy-start | bytes 6291460
  1201.6 233.8 %copy-start.30 = (f32[256]{0:T(256)}, f32[256]{0:T(256)S(1)}, u32[]{:S(2)}) copy-start(f32[256]{0:T(256)S(1)} %broadcast_multiply_fusion.6) | copy-start | bytes 3076
  1202.0 233.4 %copy-start.32 = (f32[256]{0:T(256)}, f32[256]{0:T(256)S(1)}, u32[]{:S(2)}) copy-start(f32[256]{0:T(256)S(1)} %add_rsqrt_fusion) | copy-start | bytes 3076
  1215.8 14.1 copy-start.19
  1437.9 1.3 copy-start.6
  1439.2 6.4 copy-start.5
  1525.9 174.1 %reduce-scatter.11.cloned.1.call-start = ((), (), s32[]{:S(2)}) async-start(), calls=%async_computation.15 | async-start | bytes 10485760 | tf_op jit(solution)/shard_map/reduce_scatter | solution.py:233
  1526.0 1.6 copy-start.7
  1526.0 1.8 copy-start.10
  1526.7 265.0 %reduce-scatter.15.cloned.1.call-start = ((), (), s32[]{:S(2)}) async-start(), calls=%async_computation.17 | async-start | bytes 9437184 | tf_op jit(solution)/shard_map/reduce_scatter | solution.py:189
  1533.4 1.8 copy-start.18
  1533.5 486.4 %reduce-scatter.17.cloned.1.call-start = ((), (), s32[]{:S(2)}) async-start(), calls=%async_computation.18 | async-start | bytes 25952256 | tf_op jit(solution)/shard_map/reduce_scatter | solution.py:181
  1547.9 719.8 %reduce-scatter.13.cloned.1.call-start = ((), (), s32[]{:S(2)}) async-start(), calls=%async_computation.16 | async-start | bytes 28311552 | tf_op jit(solution)/shard_map/reduce_scatter | solution.py:253
  1547.9 153.8 %copy-start.39 = (f32[256,8]{0,1:T(8,128)S(1)}, f32[256,8]{0,1:T(8,128)}, u32[]{:S(2)}) copy-start(f32[256,8]{0,1:T(8,128)} %copy-done.38) | copy-start | bytes 24580
  1547.9 153.8 %copy-start.40 = (f32[256,8]{0,1:T(8,128)S(1)}, f32[256,8]{0,1:T(8,128)}, u32[]{:S(2)}) copy-start(f32[256,8]{0,1:T(8,128)} %get-tuple-element.279) | copy-start | bytes 24580
  1701.7 2.1 copy-start.11
  1701.7 3.3 copy-start.3
  1701.7 3.3 copy-start.23
  1701.7 3.3 copy-start.27
  1701.7 3.2 copy-start.35
  1701.7 3.2 copy-start.37
  1703.6 1.0 copy-start.13
  1703.8 1.2 copy-start.15
  1720.0 1.6 copy-start.1
  1720.0 1.6 copy-start.25
  1720.0 1.6 copy-start.29
  1720.0 1.6 copy-start.31
  1720.0 1.6 copy-start.33
  1720.0 992.2 %reduce-scatter.19.cloned.1.call-start = ((), (), s32[]{:S(2)}) async-start(), calls=%async_computation.19 | async-start | bytes 51904512
  1742.9 1215.4 %all-reduce.11.cloned.1.call-start = ((), (), s32[]{:S(2)}) async-start(), calls=%async_computation.20 | async-start | bytes 25690112 | tf_op jit(solution)/shard_map/psum | solution.py:281
  2714.7 13.8 copy-start.12
  2714.7 13.8 copy-start.14
  2714.8 13.8 copy-start.16
  2729.6 14.0 copy-start.41
  2729.6 14.0 copy-start.42
  2729.6 53.9 %copy-start.8 = (f32[256,2048]{1,0:T(8,128)S(1)}, f32[256,2048]{1,0:T(8,128)}, u32[]{:S(2)}) copy-start(f32[256,2048]{1,0:T(8,128)} %copy-done.6) | copy-start | bytes 6291460
  2958.4 7.1 slice-start
  2958.4 5.5 copy-start.21
  2958.4 7.1 slice-start.1
  2965.4 5.9 copy-start.20
  (3 other events, 2.5 us)
Sparse Core Ops, SparseCore 0:
  9.7 222.6 all-gather.12
  248.2 50.6 all-gather.14
  301.3 52.4 all-gather.16
  355.3 167.6 all-gather.18
  524.5 463.9 all-gather.20
  990.0 228.3 all-gather.22
  1220.0 201.5 all-gather.24
  1526.0 84.4 reduce-scatter.8
  1613.6 86.2 reduce-scatter.10
  1702.1 89.5 reduce-scatter.14
  1794.0 225.7 reduce-scatter.16
  2022.1 245.5 reduce-scatter.12
  2270.1 442.0 reduce-scatter.18
  2716.0 242.3 all-reduce.10
